TPU v7x, 32 devices: a whole 2x2x4 slice. The times are simulated.
32 devices in a mesh: dp: 8 (over z, core), tensor: 4 (over y, x).
Axes of the slice: x: 2, y: 2, z: 4, core: 2. Of those that a mesh axis runs over, the one named last changes fastest.
Arguments:
- tokens: bfloat16 [16, 512, 1024], P('dp', 'tensor'), may hold values from -8.5 to 8.5
- segment_ids: int32 [16, 512], P('dp'), may hold values from 0 to 5, never falling along the last dimension, each value on 1 to 128 neighbouring positions
- w_qkv: bfloat16 [3, 1024, 1024], P(None, 'dp', 'tensor'), may hold values from -0.2625 to 0.2625
- w_out: bfloat16 [1024, 1024], P('tensor', 'dp'), may hold values from -1.75 to 1.75
- w_up: bfloat16 [1024, 4096], P('dp', 'tensor'), may hold values from -0.1875 to 0.1875
- w_down: bfloat16 [4096, 1024], P('tensor', 'dp'), may hold values from -0.09375 to 0.09375
- vectors: bfloat16 [12, 1024], P(None, 'dp'), may hold values from -3 to 3
- cotangent: bfloat16 [16, 512, 1024], P('dp', 'tensor'), may hold values from -6 to 6
Outputs:
- out_tokens: bfloat16 [16, 512, 1024], P('dp', 'tensor')
- grad_tokens: float32 [16, 512, 1024], P('dp', 'tensor')
- grad_qkv: float32 [3, 1024, 1024], P(None, 'dp', 'tensor')
- grad_out: float32 [1024, 1024], P('tensor', 'dp')
- grad_up: float32 [1024, 4096], P('dp', 'tensor')
- grad_down: float32 [4096, 1024], P('tensor', 'dp')
- grad_vectors: float32 [12, 1024], P(None, 'dp')
Inputs may be any that keep to these rules, and one draw needn't show every extreme that they name: `segment_ids`: within a sequence the ids never fall; each document has 1 to 128 tokens and one has exactly that many.
All inputs are finite; a program needn't handle non-finite values.
Results may differ from a plain program's by a relative error of at most 0.02.
Values may be sent and summed in bfloat16 or wider, within the bound.
A program may use at most 128 MiB of HBM per device.

v0:
```python
import jax
import jax.numpy as jnp
from jax import lax
from jax.sharding import PartitionSpec as P

D = 1024
FF = 4096
HD = 64
NORM_EPS = 1e-06
SQRT_HALF = 0.7071067811865476
INV_ROOT_TAU = 0.3989422804014327
MASKED = -1e30


def gelu_value(pre_act):
    return 0.5 * pre_act * (1.0 + lax.erf(pre_act * SQRT_HALF))


def gelu_slope(pre_act):
    return 0.5 * (1.0 + lax.erf(pre_act * SQRT_HALF)) + pre_act * INV_ROOT_TAU * jnp.exp(
        -0.5 * pre_act * pre_act
    )


def norm_forward(summed, gain, shift):
    centred = summed - jnp.mean(summed, axis=-1, keepdims=True)
    inverse = lax.rsqrt(jnp.mean(centred * centred, axis=-1, keepdims=True) + NORM_EPS)
    normed = centred * inverse
    return (normed * gain + shift, normed, inverse)


def norm_backward(normed, inverse, grad_normed):
    first_mean = jnp.mean(grad_normed, axis=-1, keepdims=True)
    second_mean = jnp.mean(grad_normed * normed, axis=-1, keepdims=True)
    return inverse * (grad_normed - first_mean - normed * second_mean)


def attention_scores(query_heads, key_heads, segments):
    same_doc = segments[:, None] == segments[None, :]
    scores = jnp.einsum(
        "qhe,khe->hqk", query_heads, key_heads, preferred_element_type=jnp.float32
    ) * HD ** (-0.5)
    return jnp.where(same_doc[None], scores, MASKED)


def collect(w_qkv, w_out, w_up, w_down, vectors):
    return (
        lax.all_gather(w_qkv, "dp", axis=1, tiled=True),
        lax.all_gather(w_out, "dp", axis=1, tiled=True),
        lax.all_gather(w_up, "dp", axis=0, tiled=True),
        lax.all_gather(w_down, "dp", axis=1, tiled=True),
        lax.all_gather(vectors, "dp", axis=1, tiled=True),
    )


def share(gradients):
    return (
        lax.psum_scatter(
            gradients[0].astype(jnp.bfloat16), "dp", scatter_dimension=1, tiled=True
        ).astype(jnp.float32),
        lax.psum_scatter(
            gradients[1].astype(jnp.bfloat16), "dp", scatter_dimension=1, tiled=True
        ).astype(jnp.float32),
        lax.psum_scatter(
            gradients[2].astype(jnp.bfloat16), "dp", scatter_dimension=0, tiled=True
        ).astype(jnp.float32),
        lax.psum_scatter(
            gradients[3].astype(jnp.bfloat16), "dp", scatter_dimension=1, tiled=True
        ).astype(jnp.float32),
        lax.psum_scatter(
            gradients[4].astype(jnp.bfloat16), "dp", scatter_dimension=1, tiled=True
        ).astype(jnp.float32),
    )


def body(tokens, segment_ids, w_qkv, w_out, w_up, w_down, vectors, cotangent):
    tensor_rank = lax.axis_index("tensor")
    local_cols = w_qkv.shape[2]
    head_count = local_cols // HD
    hidden = w_up.shape[1]
    col_start = tensor_rank * local_cols
    ffn_start = tensor_rank * hidden

    def forward(weights, tok_block, segments):
        qkv_w, out_w, up_w, down_w, vec_b = weights
        vec_f32 = vec_b.astype(jnp.float32)
        whole = lax.all_gather(tok_block, "tensor", axis=0, tiled=True)
        seq_len = whole.shape[0]
        projected = jnp.einsum("sd,tdc->tsc", whole, qkv_w, preferred_element_type=jnp.float32)
        bias_q = lax.dynamic_slice_in_dim(vec_f32[0], col_start, local_cols)
        bias_v = lax.dynamic_slice_in_dim(vec_f32[1], col_start, local_cols)
        query_heads = (projected[0] + bias_q).astype(jnp.bfloat16).reshape(seq_len, head_count, HD)
        key_heads = projected[1].astype(jnp.bfloat16).reshape(seq_len, head_count, HD)
        value_heads = (projected[2] + bias_v).astype(jnp.bfloat16).reshape(seq_len, head_count, HD)
        scores = attention_scores(query_heads, key_heads, segments)
        row_top = jnp.max(scores, axis=-1, keepdims=True)
        log_total = row_top + jnp.log(jnp.sum(jnp.exp(scores - row_top), axis=-1, keepdims=True))
        attn_probs = jnp.exp(scores - log_total).astype(jnp.bfloat16)
        context = jnp.einsum(
            "hqk,khe->qhe", attn_probs, value_heads, preferred_element_type=jnp.float32
        )
        context = context.reshape(seq_len, local_cols).astype(jnp.bfloat16)
        piece = context
        attn_mixed = lax.psum_scatter(
            jnp.dot(piece, out_w, preferred_element_type=jnp.float32).astype(jnp.bfloat16),
            "tensor",
            scatter_dimension=0,
            tiled=True,
        ).astype(jnp.float32)
        summed_one = tok_block.astype(jnp.float32) + attn_mixed + vec_f32[2]
        normed_out, normed_one, inverse_one = norm_forward(summed_one, vec_f32[3], vec_f32[4])
        normed_b = normed_out.astype(jnp.bfloat16)
        normed_whole = lax.all_gather(normed_b, "tensor", axis=0, tiled=True)
        bias_up = lax.dynamic_slice_in_dim(vec_f32[8:12].reshape(FF), ffn_start, hidden)
        pre_act = jnp.dot(normed_whole, up_w, preferred_element_type=jnp.float32) + bias_up
        activated = gelu_value(pre_act).astype(jnp.bfloat16)
        piece = activated
        summed_two = (
            normed_out
            + lax.psum_scatter(
                jnp.dot(piece, down_w, preferred_element_type=jnp.float32).astype(jnp.bfloat16),
                "tensor",
                scatter_dimension=0,
                tiled=True,
            ).astype(jnp.float32)
            + vec_f32[5]
        )
        final, normed_two, inverse_two = norm_forward(summed_two, vec_f32[6], vec_f32[7])
        saved = (
            whole,
            query_heads,
            key_heads,
            value_heads,
            log_total,
            context,
            normed_one,
            inverse_one,
            normed_whole,
            pre_act,
            activated,
            normed_two,
            inverse_two,
        )
        return (final.astype(jnp.bfloat16), saved)

    def backward(weights, saved, segments, grad_block):
        qkv_w, out_w, up_w, down_w, vec_b = weights
        vec_f32 = vec_b.astype(jnp.float32)
        (
            whole,
            query_heads,
            key_heads,
            value_heads,
            log_total,
            context,
            normed_one,
            inverse_one,
            normed_whole,
            pre_act,
            activated,
            normed_two,
            inverse_two,
        ) = saved
        seq_len = whole.shape[0]
        grad_final = grad_block.astype(jnp.float32)
        g_gain2 = jnp.sum(grad_final * normed_two, axis=0)
        g_shift2 = jnp.sum(grad_final, axis=0)
        grad_two = norm_backward(normed_two, inverse_two, grad_final * vec_f32[6])
        grad_two_b = grad_two.astype(jnp.bfloat16)
        g_bdown = jnp.sum(grad_two, axis=0)
        grad_two_whole = lax.all_gather(grad_two_b, "tensor", axis=0, tiled=True)
        g_down = jnp.dot(activated.T, grad_two_whole, preferred_element_type=jnp.float32)
        grad_pre = jnp.dot(
            grad_two_whole, down_w.T, preferred_element_type=jnp.float32
        ) * gelu_slope(pre_act)
        grad_pre_b = grad_pre.astype(jnp.bfloat16)
        g_bup = jnp.sum(grad_pre, axis=0)
        g_up = jnp.dot(normed_whole.T, grad_pre_b, preferred_element_type=jnp.float32)
        piece = grad_pre_b
        grad_one_in = grad_two + lax.psum_scatter(
            jnp.dot(piece, up_w.T, preferred_element_type=jnp.float32).astype(jnp.bfloat16),
            "tensor",
            scatter_dimension=0,
            tiled=True,
        ).astype(jnp.float32)
        g_gain1 = jnp.sum(grad_one_in * normed_one, axis=0)
        g_shift1 = jnp.sum(grad_one_in, axis=0)
        grad_one = norm_backward(normed_one, inverse_one, grad_one_in * vec_f32[3])
        grad_one_b = grad_one.astype(jnp.bfloat16)
        g_bout = jnp.sum(grad_one, axis=0)
        grad_one_whole = lax.all_gather(grad_one_b, "tensor", axis=0, tiled=True)
        g_out = jnp.dot(context.T, grad_one_whole, preferred_element_type=jnp.float32)
        grad_context = jnp.dot(grad_one_whole, out_w.T, preferred_element_type=jnp.float32).astype(
            jnp.bfloat16
        )
        grad_context = grad_context.reshape(seq_len, head_count, HD)
        scores = attention_scores(query_heads, key_heads, segments)
        attn_exact = jnp.exp(scores - log_total)
        attn_probs = attn_exact.astype(jnp.bfloat16)
        grad_probs = jnp.einsum(
            "qhe,khe->hqk", grad_context, value_heads, preferred_element_type=jnp.float32
        )
        row_dot = jnp.sum(attn_exact * grad_probs, axis=-1, keepdims=True)
        grad_scores = (attn_exact * (grad_probs - row_dot) * HD ** (-0.5)).astype(jnp.bfloat16)
        grad_value = jnp.einsum(
            "hqk,qhe->khe", attn_probs, grad_context, preferred_element_type=jnp.float32
        )
        grad_value = grad_value.reshape(seq_len, local_cols)
        grad_query = jnp.einsum(
            "hqk,khe->qhe", grad_scores, key_heads, preferred_element_type=jnp.float32
        )
        grad_query = grad_query.reshape(seq_len, local_cols)
        grad_key = jnp.einsum(
            "hqk,qhe->khe", grad_scores, query_heads, preferred_element_type=jnp.float32
        )
        grad_key = grad_key.reshape(seq_len, local_cols)
        grad_qkv = jnp.stack([grad_query, grad_key, grad_value]).astype(jnp.bfloat16)
        g_qkv = jnp.einsum("sd,tsc->tdc", whole, grad_qkv, preferred_element_type=jnp.float32)
        piece = grad_qkv
        grad_input = grad_one + lax.psum_scatter(
            jnp.einsum("tsc,tdc->sd", piece, qkv_w, preferred_element_type=jnp.float32).astype(
                jnp.bfloat16
            ),
            "tensor",
            scatter_dimension=0,
            tiled=True,
        ).astype(jnp.float32)
        zero_row = jnp.zeros((D,), jnp.float32)
        row_q = lax.dynamic_update_slice_in_dim(zero_row, jnp.sum(grad_query, axis=0), col_start, 0)
        row_v = lax.dynamic_update_slice_in_dim(zero_row, jnp.sum(grad_value, axis=0), col_start, 0)
        up_rows = lax.dynamic_update_slice_in_dim(
            jnp.zeros((FF,), jnp.float32), g_bup, ffn_start, 0
        ).reshape(4, D)
        first_rows = jnp.stack(
            [row_q, row_v, g_bout, g_gain1, g_shift1, g_bdown, g_gain2, g_shift2]
        )
        g_vec = jnp.concatenate([first_rows, up_rows], axis=0)
        return ((g_qkv, g_out, g_up, g_down, g_vec), grad_input)

    def one_batch(carried, batch_item):
        tok_block, segments, grad_block = batch_item
        forward_w = collect(w_qkv, w_out, w_up, w_down, vectors)
        final_b, saved = forward(forward_w, tok_block, segments)
        second = collect(w_qkv, w_out, w_up, w_down, vectors)
        gradients, grad_input = backward(second, saved, segments, grad_block)
        updated = jax.tree.map(jnp.add, carried, gradients)
        return (updated, (final_b, grad_input))

    initial = (
        jnp.zeros((3, D, local_cols), jnp.float32),
        jnp.zeros((local_cols, D), jnp.float32),
        jnp.zeros((D, hidden), jnp.float32),
        jnp.zeros((hidden, D), jnp.float32),
        jnp.zeros((12, D), jnp.float32),
    )
    carried, stacked = lax.scan(one_batch, initial, (tokens, segment_ids, cotangent))
    totals = share(carried)
    vector_grads = lax.psum(totals[4], "tensor")
    return (stacked[0], stacked[1], totals[0], totals[1], totals[2], totals[3], vector_grads)


def solution(mesh):
    return jax.shard_map(
        body,
        mesh=mesh,
        in_specs=(
            P("dp", "tensor", None),
            P("dp", None),
            P(None, "dp", "tensor"),
            P("tensor", "dp"),
            P("dp", "tensor"),
            P("tensor", "dp"),
            P(None, "dp"),
            P("dp", "tensor", None),
        ),
        out_specs=(
            P("dp", "tensor", None),
            P("dp", "tensor", None),
            P(None, "dp", "tensor"),
            P("tensor", "dp"),
            P("dp", "tensor"),
            P("tensor", "dp"),
            P(None, "dp"),
        ),
        check_vma=False,
    )
```

profile of v0, /device:TPU:0, one launch (start us, length us, event | category | flops | bytes accessed | tf_op | source)
XLA Modules:
  0.0 942.0 jit_solution(16017847547988003658)
XLA Ops:
  9.8 748.5 %while.25 = (s32[]{:T(128)}, f32[3,1024,256]{1,2,0:T(8,128)}, f32[256,1024]{1,0:T(8,128)}, f32[1024,1024]{1,0:T(8,128)}, f32[1024,1024]{1,0:T(8,128)}, /*index=5...) while((s32[]{:T(128)}, f32[3,1024,256]{1,2,0:T(8,128)}, ...), condition=%wide.region_25.26_spmd.clone, body=%wide.region_0.25_spmd.clone.sunk | while | flops 10544906240 | bytes 269724672 | solution.py:256
  12.3 14.6 %all_gather.66 = bf16[12,1024]{1,0:T(8,128)(2,1)S(1)} all-gather(bf16[12,128]{1,0:T(8,128)(2,1)} %get-tuple-element.627), channel_id=1, replica_groups=mesh['dp'=8,'tensor'=4] {'dp'}, dimensions={1}, use_global_device_ids=true | all-gather | bytes 27648 | tf_op jit(solution)/shard_map/while/body/eval_jaxpr/all_gather | solution.py:52
  27.9 13.9 %all_gather.69 = bf16[256,1024]{1,0:T(8,128)(2,1)S(1)} all-gather(bf16[256,128]{1,0:T(8,128)(2,1)} %get-tuple-element.629), channel_id=1, replica_groups=mesh['dp'=8,'tensor'=4] {'dp'}, dimensions={1}, use_global_device_ids=true | all-gather | bytes 589824 | tf_op jit(solution)/shard_map/while/body/eval_jaxpr/all_gather | solution.py:49
  42.3 28.7 %all-gather.16.cloned.1.call-done = bf16[3,1024,256]{1,2,0:T(8,128)(2,1)} async-done(((bf16[3,128,256]{1,2,0:T(8,128)(2,1)}), bf16[3,1024,256]{1,2,0:T(8,128)(2,1)}) %all-gather.16.cloned.1.call-update) | async-done | bytes 1572880 | tf_op jit(solution)/shard_map/while/body/eval_jaxpr/all_gather | solution.py:48
  71.0 2.7 convolution_bitcast_fusion.3
  79.2 26.3 %reduce-scatter.26.cloned.1.call-done = bf16[128,1024]{1,0:T(8,128)(2,1)} async-done(((bf16[512,1024]{1,0:T(8,128)(2,1)}), bf16[128,1024]{1,0:T(8,128)(2,1)}) %reduce-scatter.26.cloned.1.call-update) | async-done | bytes 262160 | tf_op jit(solution)/shard_map/while/body/eval_jaxpr/reduce_scatter | solution.py:104
  110.3 25.8 %all-gather.20.cloned.1.call-done = bf16[1024,1024]{1,0:T(8,128)(2,1)} async-done(((bf16[128,1024]{1,0:T(8,128)(2,1)}), bf16[1024,1024]{1,0:T(8,128)(2,1)}) %all-gather.20.cloned.1.call-update) | async-done | bytes 2097168 | tf_op jit(solution)/shard_map/while/body/eval_jaxpr/all_gather | solution.py:50
  136.2 28.2 %all-gather.18.cloned.1.call-done = bf16[512,1024]{1,0:T(8,128)(2,1)} async-done(((bf16[128,1024]{1,0:T(8,128)(2,1)}), bf16[512,1024]{1,0:T(8,128)(2,1)}) %all-gather.18.cloned.1.call-update) | async-done | bytes 1048592 | tf_op jit(solution)/shard_map/while/body/eval_jaxpr/all_gather | solution.py:113
  164.4 4.5 fusion.165
  168.9 27.5 %all-gather.14.cloned.1.call-done = bf16[1024,1024]{1,0:T(8,128)(2,1)} async-done(((bf16[1024,128]{1,0:T(8,128)(2,1)}), bf16[1024,1024]{1,0:T(8,128)(2,1)}) %all-gather.14.cloned.1.call-update) | async-done | bytes 2097168 | tf_op jit(solution)/shard_map/while/body/eval_jaxpr/all_gather | solution.py:51
  196.5 4.5 convolution_convert_fusion.12
  201.0 27.1 %reduce-scatter.28.cloned.1.call-done = bf16[128,1024]{1,0:T(8,128)(2,1)} async-done(((bf16[512,1024]{1,0:T(8,128)(2,1)}), bf16[128,1024]{1,0:T(8,128)(2,1)}) %reduce-scatter.28.cloned.1.call-update) | async-done | bytes 262160 | tf_op jit(solution)/shard_map/while/body/eval_jaxpr/reduce_scatter | solution.py:120
  232.4 26.6 %all-gather.22.cloned.1.call-done = bf16[512,1024]{1,0:T(8,128)(2,1)} async-done(((bf16[128,1024]{1,0:T(8,128)(2,1)}), bf16[512,1024]{1,0:T(8,128)(2,1)}) %all-gather.22.cloned.1.call-update) | async-done | bytes 1048592 | tf_op jit(solution)/shard_map/while/body/eval_jaxpr/all_gather | solution.py:171
  259.0 4.6 fusion.169
  264.5 2.3 convolution_convert_fusion.13
  266.9 28.0 %reduce-scatter.30.cloned.1.call-done = bf16[128,1024]{1,0:T(8,128)(2,1)} async-done(((bf16[512,1024]{1,0:T(8,128)(2,1)}), bf16[128,1024]{1,0:T(8,128)(2,1)}) %reduce-scatter.30.cloned.1.call-update) | async-done | bytes 262160 | tf_op jit(solution)/shard_map/while/body/eval_jaxpr/reduce_scatter | solution.py:180
  303.1 23.9 %all-gather.24.cloned.1.call-done = bf16[512,1024]{1,0:T(8,128)(2,1)} async-done(((bf16[128,1024]{1,0:T(8,128)(2,1)}), bf16[512,1024]{1,0:T(8,128)(2,1)}) %all-gather.24.cloned.1.call-update) | async-done | bytes 1048592 | tf_op jit(solution)/shard_map/while/body/eval_jaxpr/all_gather | solution.py:191
  328.7 3.5 fusion.171
  332.2 2.9 fusion.172
  335.0 8.1 fusion.173
  343.1 8.8 fusion.174
  351.9 3.6 bitcast_convert_fusion.2
  355.6 3.3 select_add_fusion.6
  358.8 3.3 select_add_fusion.7
  365.0 2.7 convolution_add_fusion.2
  367.6 3.0 bitcast_add_fusion.2
  370.7 12.9 %reduce-scatter.32.cloned.1.call-done = bf16[128,1024]{1,0:T(8,128)(2,1)} async-done(((bf16[512,1024]{1,0:T(8,128)(2,1)}), bf16[128,1024]{1,0:T(8,128)(2,1)}) %reduce-scatter.32.cloned.1.call-update) | async-done | bytes 262160 | tf_op jit(solution)/shard_map/while/body/eval_jaxpr/reduce_scatter | solution.py:220
  388.1 13.0 %all_gather.66 = bf16[12,1024]{1,0:T(8,128)(2,1)S(1)} all-gather(bf16[12,128]{1,0:T(8,128)(2,1)} %get-tuple-element.627), channel_id=1, replica_groups=mesh['dp'=8,'tensor'=4] {'dp'}, dimensions={1}, use_global_device_ids=true | all-gather | bytes 27648 | tf_op jit(solution)/shard_map/while/body/eval_jaxpr/all_gather | solution.py:52
  402.0 14.0 %all_gather.69 = bf16[256,1024]{1,0:T(8,128)(2,1)S(1)} all-gather(bf16[256,128]{1,0:T(8,128)(2,1)} %get-tuple-element.629), channel_id=1, replica_groups=mesh['dp'=8,'tensor'=4] {'dp'}, dimensions={1}, use_global_device_ids=true | all-gather | bytes 589824 | tf_op jit(solution)/shard_map/while/body/eval_jaxpr/all_gather | solution.py:49
  416.2 27.5 %all-gather.16.cloned.1.call-done = bf16[3,1024,256]{1,2,0:T(8,128)(2,1)} async-done(((bf16[3,128,256]{1,2,0:T(8,128)(2,1)}), bf16[3,1024,256]{1,2,0:T(8,128)(2,1)}) %all-gather.16.cloned.1.call-update) | async-done | bytes 1572880 | tf_op jit(solution)/shard_map/while/body/eval_jaxpr/all_gather | solution.py:48
  443.7 2.7 convolution_bitcast_fusion.3
  452.0 26.3 %reduce-scatter.26.cloned.1.call-done = bf16[128,1024]{1,0:T(8,128)(2,1)} async-done(((bf16[512,1024]{1,0:T(8,128)(2,1)}), bf16[128,1024]{1,0:T(8,128)(2,1)}) %reduce-scatter.26.cloned.1.call-update) | async-done | bytes 262160 | tf_op jit(solution)/shard_map/while/body/eval_jaxpr/reduce_scatter | solution.py:104
  483.1 25.8 %all-gather.20.cloned.1.call-done = bf16[1024,1024]{1,0:T(8,128)(2,1)} async-done(((bf16[128,1024]{1,0:T(8,128)(2,1)}), bf16[1024,1024]{1,0:T(8,128)(2,1)}) %all-gather.20.cloned.1.call-update) | async-done | bytes 2097168 | tf_op jit(solution)/shard_map/while/body/eval_jaxpr/all_gather | solution.py:50
  508.9 28.2 %all-gather.18.cloned.1.call-done = bf16[512,1024]{1,0:T(8,128)(2,1)} async-done(((bf16[128,1024]{1,0:T(8,128)(2,1)}), bf16[512,1024]{1,0:T(8,128)(2,1)}) %all-gather.18.cloned.1.call-update) | async-done | bytes 1048592 | tf_op jit(solution)/shard_map/while/body/eval_jaxpr/all_gather | solution.py:113
  537.1 4.5 fusion.165
  541.6 27.5 %all-gather.14.cloned.1.call-done = bf16[1024,1024]{1,0:T(8,128)(2,1)} async-done(((bf16[1024,128]{1,0:T(8,128)(2,1)}), bf16[1024,1024]{1,0:T(8,128)(2,1)}) %all-gather.14.cloned.1.call-update) | async-done | bytes 2097168 | tf_op jit(solution)/shard_map/while/body/eval_jaxpr/all_gather | solution.py:51
  569.1 4.5 convolution_convert_fusion.12
  573.7 27.1 %reduce-scatter.28.cloned.1.call-done = bf16[128,1024]{1,0:T(8,128)(2,1)} async-done(((bf16[512,1024]{1,0:T(8,128)(2,1)}), bf16[128,1024]{1,0:T(8,128)(2,1)}) %reduce-scatter.28.cloned.1.call-update) | async-done | bytes 262160 | tf_op jit(solution)/shard_map/while/body/eval_jaxpr/reduce_scatter | solution.py:120
  605.0 26.6 %all-gather.22.cloned.1.call-done = bf16[512,1024]{1,0:T(8,128)(2,1)} async-done(((bf16[128,1024]{1,0:T(8,128)(2,1)}), bf16[512,1024]{1,0:T(8,128)(2,1)}) %all-gather.22.cloned.1.call-update) | async-done | bytes 1048592 | tf_op jit(solution)/shard_map/while/body/eval_jaxpr/all_gather | solution.py:171
  631.7 4.6 fusion.169
  637.2 2.3 convolution_convert_fusion.13
  639.6 28.0 %reduce-scatter.30.cloned.1.call-done = bf16[128,1024]{1,0:T(8,128)(2,1)} async-done(((bf16[512,1024]{1,0:T(8,128)(2,1)}), bf16[128,1024]{1,0:T(8,128)(2,1)}) %reduce-scatter.30.cloned.1.call-update) | async-done | bytes 262160 | tf_op jit(solution)/shard_map/while/body/eval_jaxpr/reduce_scatter | solution.py:180
  675.8 23.9 %all-gather.24.cloned.1.call-done = bf16[512,1024]{1,0:T(8,128)(2,1)} async-done(((bf16[128,1024]{1,0:T(8,128)(2,1)}), bf16[512,1024]{1,0:T(8,128)(2,1)}) %all-gather.24.cloned.1.call-update) | async-done | bytes 1048592 | tf_op jit(solution)/shard_map/while/body/eval_jaxpr/all_gather | solution.py:191
  701.3 3.5 fusion.171
  704.8 2.9 fusion.172
  707.7 8.1 fusion.173
  715.8 8.8 fusion.174
  724.6 3.6 bitcast_convert_fusion.2
  728.2 5.6 select_add_fusion.6
  733.9 5.7 select_add_fusion.7
  742.3 3.0 convolution_add_fusion.2
  745.3 2.9 bitcast_add_fusion.2
  748.3 8.0 reduce-scatter.32.cloned.1.call-done
  759.3 2.1 convert_element_type.170
  761.4 2.0 copy.37
  765.4 2.5 convert_element_type.174
  767.9 2.6 copy.39
  770.6 3.9 convert_element_type.172
  774.5 17.9 %reduce-scatter.24.cloned.1.call-done = bf16[128,12]{1,0:T(8,128)(2,1)} async-done(((bf16[1024,12]{1,0:T(8,128)(2,1)}), bf16[128,12]{1,0:T(8,128)(2,1)}) %reduce-scatter.24.cloned.1.call-update) | async-done | bytes 3088
  793.2 10.6 %psum.7 = f32[12,128]{1,0:T(8,128)} all-reduce(bf16[12,128]{1,0:T(8,128)(2,1)S(1)} %copy.42), channel_id=1, replica_groups=mesh['dp'=8,'tensor'=4] {'tensor'}, use_global_device_ids=true, to_apply=%region_31.32 | all-reduce | flops 1536 | bytes 9216 | tf_op jit(solution)/shard_map/psum | solution.py:258
  803.8 20.7 %reduce-scatter.20.cloned.1.call-done = bf16[128,256]{1,0:T(8,128)(2,1)} async-done(((bf16[1024,256]{1,0:T(8,128)(2,1)}), bf16[128,256]{1,0:T(8,128)(2,1)}) %reduce-scatter.20.cloned.1.call-update) | async-done | bytes 65552
  826.1 32.9 %reduce-scatter.16.cloned.1.call-done = bf16[3,128,256]{2,1,0:T(8,128)(2,1)} async-done(((bf16[3,1024,256]{2,1,0:T(8,128)(2,1)}), bf16[3,128,256]{2,1,0:T(8,128)(2,1)}) %reduce-scatter.16.cloned.1.call-update) | async-done | bytes 196624 | tf_op jit(solution)/shard_map/reduce_scatter | solution.py:58
  860.7 35.1 %reduce-scatter.22.cloned.1.call-done = bf16[128,1024]{1,0:T(8,128)(2,1)} async-done(((bf16[1024,1024]{1,0:T(8,128)(2,1)}), bf16[128,1024]{1,0:T(8,128)(2,1)}) %reduce-scatter.22.cloned.1.call-update) | async-done | bytes 262160
  897.7 34.9 %reduce-scatter.18.cloned.1.call-done = bf16[128,1024]{1,0:T(8,128)(2,1)} async-done(((bf16[1024,1024]{1,0:T(8,128)(2,1)}), bf16[128,1024]{1,0:T(8,128)(2,1)}) %reduce-scatter.18.cloned.1.call-update) | async-done | bytes 262160 | tf_op jit(solution)/shard_map/reduce_scatter | solution.py:64
  (286 shorter events, 80.1 us)
Async XLA Ops:
  9.8 32.5 %all-gather.12.cloned.1.call-start = ((), (), s32[]{:S(2)}) async-start(), calls=%async_computation.14 | async-start | bytes 1310720 | tf_op jit(solution)/shard_map/while/body/eval_jaxpr/all_gather | solution.py:87
  11.5 59.5 %all-gather.16.cloned.1.call-start = ((), (), s32[]{:S(2)}) async-start(), calls=%async_computation.16 | async-start | bytes 1769472 | tf_op jit(solution)/shard_map/while/body/eval_jaxpr/all_gather | solution.py:48
  12.3 93.2 %reduce-scatter.26.cloned.1.call-start = ((), (), s32[]{:S(2)}) async-start(), calls=%async_computation.17 | async-start | bytes 1310720 | tf_op jit(solution)/shard_map/while/body/eval_jaxpr/reduce_scatter | solution.py:104
  27.1 48.7 %copy-start.23 = (f32[4,64]{1,0:T(4,128)}, f32[4,64]{1,0:T(4,128)S(1)}, u32[]{:S(2)}) copy-start(f32[4,64]{1,0:T(4,128)S(1)} %add.495) | copy-start | bytes 3076 | tf_op jit(solution)/shard_map/while
  27.2 46.7 %copy-start.21 = (f32[4,64]{1,0:T(4,128)}, f32[4,64]{1,0:T(4,128)S(1)}, u32[]{:S(2)}) copy-start(f32[4,64]{1,0:T(4,128)S(1)} %add.496) | copy-start | bytes 3076 | tf_op jit(solution)/shard_map/while
  75.8 29.7 %copy-start.5 = (bf16[2,128,1024]{2,1,0:T(8,128)(2,1)S(1)}, bf16[2,128,1024]{2,1,0:T(8,128)(2,1)}, u32[]{:S(2)}) copy-start(bf16[2,128,1024]{2,1,0:T(8,128)(2,1)} %get-tuple-element.624) | copy-start | bytes 1572868 | tf_op jit(solution)/shard_map/while
  78.6 57.6 %all-gather.20.cloned.1.call-start = ((), (), s32[]{:S(2)}) async-start(), calls=%async_computation.19 | async-start | bytes 2359296 | tf_op jit(solution)/shard_map/while/body/eval_jaxpr/all_gather | solution.py:50
  79.2 85.2 %all-gather.18.cloned.1.call-start = ((), (), s32[]{:S(2)}) async-start(), calls=%async_computation.18 | async-start | bytes 1310720 | tf_op jit(solution)/shard_map/while/body/eval_jaxpr/all_gather | solution.py:113
  109.7 86.8 %all-gather.14.cloned.1.call-start = ((), (), s32[]{:S(2)}) async-start(), calls=%async_computation.15 | async-start | bytes 2359296 | tf_op jit(solution)/shard_map/while/body/eval_jaxpr/all_gather | solution.py:51
  110.2 117.9 %reduce-scatter.28.cloned.1.call-start = ((), (), s32[]{:S(2)}) async-start(), calls=%async_computation.20 | async-start | bytes 1310720 | tf_op jit(solution)/shard_map/while/body/eval_jaxpr/reduce_scatter | solution.py:120
  168.9 59.2 %copy-start.1 = (bf16[128,1024]{1,0:T(8,128)(2,1)S(1)}, bf16[128,1024]{1,0:T(8,128)(2,1)}, u32[]{:S(2)}) copy-start(bf16[128,1024]{1,0:T(8,128)(2,1)} %reduce-scatter.26.cloned.1.call-done) | copy-start | bytes 786436 | tf_op jit(solution)/shard_map/while
  168.9 60.7 %copy-start.11 = (bf16[2,128,1024]{2,1,0:T(8,128)(2,1)S(1)}, bf16[2,128,1024]{2,1,0:T(8,128)(2,1)}, u32[]{:S(2)}) copy-start(bf16[2,128,1024]{2,1,0:T(8,128)(2,1)} %get-tuple-element.633) | copy-start | bytes 1572868 | tf_op jit(solution)/shard_map/while
  201.0 58.0 %all-gather.22.cloned.1.call-start = ((), (), s32[]{:S(2)}) async-start(), calls=%async_computation.21 | async-start | bytes 1310720 | tf_op jit(solution)/shard_map/while/body/eval_jaxpr/all_gather | solution.py:171
  232.3 62.6 %reduce-scatter.30.cloned.1.call-start = ((), (), s32[]{:S(2)}) async-start(), calls=%async_computation.22 | async-start | bytes 1310720 | tf_op jit(solution)/shard_map/while/body/eval_jaxpr/reduce_scatter | solution.py:180
  259.0 5.6 copy-start.27
  266.9 61.8 %copy-start.26 = (f32[4,512]{1,0:T(4,128)S(1)}, f32[4,512]{1,0:T(4,128)}, u32[]{:S(2)}) copy-start(f32[4,512]{1,0:T(4,128)} %copy-done.25) | copy-start | bytes 24580 | tf_op jit(solution)/shard_map/while
  266.9 60.0 %all-gather.24.cloned.1.call-start = ((), (), s32[]{:S(2)}) async-start(), calls=%async_computation.23 | async-start | bytes 1310720 | tf_op jit(solution)/shard_map/while/body/eval_jaxpr/all_gather | solution.py:191
  300.3 83.3 %reduce-scatter.32.cloned.1.call-start = ((), (), s32[]{:S(2)}) async-start(), calls=%async_computation.24 | async-start | bytes 1310720 | tf_op jit(solution)/shard_map/while/body/eval_jaxpr/reduce_scatter | solution.py:220
  302.8 29.3 %copy-start.9 = (f32[1,512,256]{1,2,0:T(8,128)S(1)}, f32[1,512,256]{1,2,0:T(8,128)}, u32[]{:S(2)}) copy-start(f32[1,512,256]{1,2,0:T(8,128)} %copy-done.8) | copy-start | bytes 1572868 | tf_op jit(solution)/shard_map/while
  302.8 29.4 %copy-start.24 = (f32[4,64]{1,0:T(4,128)S(1)}, f32[4,64]{1,0:T(4,128)}, u32[]{:S(2)}) copy-start(f32[4,64]{1,0:T(4,128)} %copy-done.23) | copy-start | bytes 3076 | tf_op jit(solution)/shard_map/while
  328.7 6.4 copy-start.22
  332.1 19.8 %copy-start.17 = (bf16[512,4,64]{0,2,1:T(8,128)(2,1)}, bf16[512,4,64]{0,2,1:T(8,128)(2,1)S(1)}, u32[]{:S(2)}) copy-start(bf16[512,4,64]{0,2,1:T(8,128)(2,1)S(1)} %get-tuple-element.563) | copy-start | bytes 786436 | tf_op jit(solution)/shard_map/while
  335.0 8.1 copy-start.15
  343.1 8.8 copy-start.18
  351.9 3.6 copy-start.7
  351.9 3.6 copy-start.13
  362.2 5.5 copy-start.2
  370.6 14.9 %copy-start.3 = (f32[3,1024,256]{1,2,0:T(8,128)}, f32[3,1024,256]{1,2,0:T(8,128)S(1)}, u32[]{:S(2)}) copy-start(f32[3,1024,256]{1,2,0:T(8,128)S(1)} %bitcast_add_fusion.2) | copy-start | bytes 9437188 | tf_op jit(solution)/shard_map/while
  385.6 30.6 %all-gather.12.cloned.1.call-start = ((), (), s32[]{:S(2)}) async-start(), calls=%async_computation.14 | async-start | bytes 1310720 | tf_op jit(solution)/shard_map/while/body/eval_jaxpr/all_gather | solution.py:87
  387.3 56.4 %all-gather.16.cloned.1.call-start = ((), (), s32[]{:S(2)}) async-start(), calls=%async_computation.16 | async-start | bytes 1769472 | tf_op jit(solution)/shard_map/while/body/eval_jaxpr/all_gather | solution.py:48
  388.0 90.2 %reduce-scatter.26.cloned.1.call-start = ((), (), s32[]{:S(2)}) async-start(), calls=%async_computation.17 | async-start | bytes 1310720 | tf_op jit(solution)/shard_map/while/body/eval_jaxpr/reduce_scatter | solution.py:104
  401.2 47.3 %copy-start.23 = (f32[4,64]{1,0:T(4,128)}, f32[4,64]{1,0:T(4,128)S(1)}, u32[]{:S(2)}) copy-start(f32[4,64]{1,0:T(4,128)S(1)} %add.495) | copy-start | bytes 3076 | tf_op jit(solution)/shard_map/while
  401.3 45.3 %copy-start.21 = (f32[4,64]{1,0:T(4,128)}, f32[4,64]{1,0:T(4,128)S(1)}, u32[]{:S(2)}) copy-start(f32[4,64]{1,0:T(4,128)S(1)} %add.496) | copy-start | bytes 3076 | tf_op jit(solution)/shard_map/while
  448.5 29.7 %copy-start.5 = (bf16[2,128,1024]{2,1,0:T(8,128)(2,1)S(1)}, bf16[2,128,1024]{2,1,0:T(8,128)(2,1)}, u32[]{:S(2)}) copy-start(bf16[2,128,1024]{2,1,0:T(8,128)(2,1)} %get-tuple-element.624) | copy-start | bytes 1572868 | tf_op jit(solution)/shard_map/while
  451.3 57.5 %all-gather.20.cloned.1.call-start = ((), (), s32[]{:S(2)}) async-start(), calls=%async_computation.19 | async-start | bytes 2359296 | tf_op jit(solution)/shard_map/while/body/eval_jaxpr/all_gather | solution.py:50
  451.9 85.1 %all-gather.18.cloned.1.call-start = ((), (), s32[]{:S(2)}) async-start(), calls=%async_computation.18 | async-start | bytes 1310720 | tf_op jit(solution)/shard_map/while/body/eval_jaxpr/all_gather | solution.py:113
  482.4 86.8 %all-gather.14.cloned.1.call-start = ((), (), s32[]{:S(2)}) async-start(), calls=%async_computation.15 | async-start | bytes 2359296 | tf_op jit(solution)/shard_map/while/body/eval_jaxpr/all_gather | solution.py:51
  483.0 117.8 %reduce-scatter.28.cloned.1.call-start = ((), (), s32[]{:S(2)}) async-start(), calls=%async_computation.20 | async-start | bytes 1310720 | tf_op jit(solution)/shard_map/while/body/eval_jaxpr/reduce_scatter | solution.py:120
  541.6 59.2 %copy-start.1 = (bf16[128,1024]{1,0:T(8,128)(2,1)S(1)}, bf16[128,1024]{1,0:T(8,128)(2,1)}, u32[]{:S(2)}) copy-start(bf16[128,1024]{1,0:T(8,128)(2,1)} %reduce-scatter.26.cloned.1.call-done) | copy-start | bytes 786436 | tf_op jit(solution)/shard_map/while
  541.6 60.7 %copy-start.11 = (bf16[2,128,1024]{2,1,0:T(8,128)(2,1)S(1)}, bf16[2,128,1024]{2,1,0:T(8,128)(2,1)}, u32[]{:S(2)}) copy-start(bf16[2,128,1024]{2,1,0:T(8,128)(2,1)} %get-tuple-element.633) | copy-start | bytes 1572868 | tf_op jit(solution)/shard_map/while
  573.7 58.0 %all-gather.22.cloned.1.call-start = ((), (), s32[]{:S(2)}) async-start(), calls=%async_computation.21 | async-start | bytes 1310720 | tf_op jit(solution)/shard_map/while/body/eval_jaxpr/all_gather | solution.py:171
  605.0 62.6 %reduce-scatter.30.cloned.1.call-start = ((), (), s32[]{:S(2)}) async-start(), calls=%async_computation.22 | async-start | bytes 1310720 | tf_op jit(solution)/shard_map/while/body/eval_jaxpr/reduce_scatter | solution.py:180
  631.7 5.6 copy-start.27
  639.5 61.8 %copy-start.26 = (f32[4,512]{1,0:T(4,128)S(1)}, f32[4,512]{1,0:T(4,128)}, u32[]{:S(2)}) copy-start(f32[4,512]{1,0:T(4,128)} %copy-done.25) | copy-start | bytes 24580 | tf_op jit(solution)/shard_map/while
  639.6 60.0 %all-gather.24.cloned.1.call-start = ((), (), s32[]{:S(2)}) async-start(), calls=%async_computation.23 | async-start | bytes 1310720 | tf_op jit(solution)/shard_map/while/body/eval_jaxpr/all_gather | solution.py:191
  673.0 83.4 %reduce-scatter.32.cloned.1.call-start = ((), (), s32[]{:S(2)}) async-start(), calls=%async_computation.24 | async-start | bytes 1310720 | tf_op jit(solution)/shard_map/while/body/eval_jaxpr/reduce_scatter | solution.py:220
  675.5 29.3 %copy-start.9 = (f32[1,512,256]{1,2,0:T(8,128)S(1)}, f32[1,512,256]{1,2,0:T(8,128)}, u32[]{:S(2)}) copy-start(f32[1,512,256]{1,2,0:T(8,128)} %copy-done.8) | copy-start | bytes 1572868 | tf_op jit(solution)/shard_map/while
  675.5 29.4 %copy-start.24 = (f32[4,64]{1,0:T(4,128)S(1)}, f32[4,64]{1,0:T(4,128)}, u32[]{:S(2)}) copy-start(f32[4,64]{1,0:T(4,128)} %copy-done.23) | copy-start | bytes 3076 | tf_op jit(solution)/shard_map/while
  701.3 6.4 copy-start.22
  704.8 19.8 %copy-start.17 = (bf16[512,4,64]{0,2,1:T(8,128)(2,1)}, bf16[512,4,64]{0,2,1:T(8,128)(2,1)S(1)}, u32[]{:S(2)}) copy-start(bf16[512,4,64]{0,2,1:T(8,128)(2,1)S(1)} %get-tuple-element.563) | copy-start | bytes 786436 | tf_op jit(solution)/shard_map/while
  707.7 8.1 copy-start.15
  715.8 8.8 copy-start.18
  724.6 3.6 copy-start.7
  724.6 3.6 copy-start.13
  728.2 5.6 copy-start.10
  728.2 5.6 copy-start.16
  739.5 5.8 copy-start.2
  748.3 10.0 %copy-start.3 = (f32[3,1024,256]{1,2,0:T(8,128)}, f32[3,1024,256]{1,2,0:T(8,128)S(1)}, u32[]{:S(2)}) copy-start(f32[3,1024,256]{1,2,0:T(8,128)S(1)} %bitcast_add_fusion.2) | copy-start | bytes 9437188 | tf_op jit(solution)/shard_map/while
  758.3 5.3 copy-start.4
  758.3 34.0 %reduce-scatter.24.cloned.1.call-start = ((), (), s32[]{:S(2)}) async-start(), calls=%async_computation.13 | async-start | bytes 294912
  759.3 65.2 %reduce-scatter.20.cloned.1.call-start = ((), (), s32[]{:S(2)}) async-start(), calls=%async_computation.11 | async-start | bytes 589824
  763.5 95.5 %reduce-scatter.16.cloned.1.call-start = ((), (), s32[]{:S(2)}) async-start(), calls=%async_computation.9 | async-start | bytes 1769472 | tf_op jit(solution)/shard_map/reduce_scatter | solution.py:58
  765.3 130.5 %reduce-scatter.22.cloned.1.call-start = ((), (), s32[]{:S(2)}) async-start(), calls=%async_computation.12 | async-start | bytes 2359296
  770.5 162.1 %reduce-scatter.18.cloned.1.call-start = ((), (), s32[]{:S(2)}) async-start(), calls=%async_computation.10 | async-start | bytes 2359296 | tf_op jit(solution)/shard_map/reduce_scatter | solution.py:64
  (18 other events, 36.7 us)
Sparse Core Ops, SparseCore 0:
  13.0 29.2 all-gather.11
  43.9 27.0 all-gather.15
  78.7 26.7 reduce-scatter.25
  107.0 29.1 all-gather.19
  138.4 25.8 all-gather.17
  165.8 30.5 all-gather.13
  201.1 26.9 reduce-scatter.27
  232.4 26.4 all-gather.21
  267.0 27.9 reduce-scatter.29
  300.4 26.4 all-gather.23
  355.6 27.9 reduce-scatter.31
  388.5 26.4 all-gather.11
  416.6 27.0 all-gather.15
  451.4 26.7 reduce-scatter.25
  479.7 29.1 all-gather.19
  511.1 25.8 all-gather.17
  538.5 30.5 all-gather.13
  573.8 26.9 reduce-scatter.27
  605.1 26.4 all-gather.21
  639.7 27.9 reduce-scatter.29
  673.1 26.4 all-gather.23
  728.3 27.9 reduce-scatter.31
Sparse Core Ops, SparseCore 1:
  761.6 30.7 reduce-scatter.23
  795.1 29.4 reduce-scatter.19
  826.7 32.3 reduce-scatter.15
  861.3 34.4 reduce-scatter.21
  898.1 34.4 reduce-scatter.17
where the time goes:
time: 944 us; the launch traced here: 942 us
  waiting for transfers between devices  649 us (69%)
  matrix products  131 us (14%)
  blocking collectives  66.2 us (7%)
  other arithmetic  50.2 us (5%)
  local copies, waits for them, and re-layouts  27.1 us (3%)
  between operations  15.8 us (2%)
    unnamed x8, waiting for transfers between devices  73.8 us
    all_gather x2, waiting for transfers between devices, forward(): normed_whole = lax.all_gather(normed_b, 'tensor', axis=0, tiled=True)  56.4 us
    all_gather x2, waiting for transfers between devices, collect(): lax.all_gather(w_qkv, 'dp', axis=1, tiled=True)  56.2 us
    reduce_scatter x2, waiting for transfers between devices, backward(): lax.psum_scatter(jnp.dot(piece, up_w.T, preferred_element_type=jnp.float3...  56.1 us
    all_gather x2, waiting for transfers between devices, collect(): lax.all_gather(w_down, 'dp', axis=1, tiled=True)  55.1 us
    reduce_scatter x2, waiting for transfers between devices, forward(): lax.psum_scatter(jnp.dot(piece, down_w, preferred_element_type=jnp.float3...  54.1 us
    all_gather x2, waiting for transfers between devices, backward(): grad_two_whole = lax.all_gather(grad_two_b, 'tensor', axis=0, tiled=True)  53.2 us
    reduce_scatter x2, waiting for transfers between devices, forward(): lax.psum_scatter(jnp.dot(piece, out_w, preferred_element_type=jnp.float32...  52.5 us
  transfers between devices with their start and end apart: 27, of which 26 were waited for; matrix products, arithmetic and copies ran while one was open for 8% of the time, Pallas kernels for 0%

commit v1 on v0

--- a/solution.py
+++ b/solution.py
@@ -12,6 +12,16 @@
 MASKED = -1e30
 
 
+def collect_2(x, axis, dim):
+    ways, here, hop = (lax.axis_size(axis), lax.axis_index(axis), x.shape[dim])
+    lengths = [n * ways if d == dim else n for d, n in enumerate(x.shape)]
+    full = lax.dynamic_update_slice_in_dim(jnp.zeros(lengths, x.dtype), x, here * hop, axis=dim)
+    for far in range(1, ways):
+        x = lax.ppermute(x, axis, [(d, (d + 1) % ways) for d in range(ways)])
+        full = lax.dynamic_update_slice_in_dim(full, x, (here - far) % ways * hop, axis=dim)
+    return full
+
+
 def gelu_value(pre_act):
     return 0.5 * pre_act * (1.0 + lax.erf(pre_act * SQRT_HALF))
 
@@ -45,7 +55,7 @@
 
 def collect(w_qkv, w_out, w_up, w_down, vectors):
     return (
-        lax.all_gather(w_qkv, "dp", axis=1, tiled=True),
+        collect_2(w_qkv, "dp", 1),
         lax.all_gather(w_out, "dp", axis=1, tiled=True),
         lax.all_gather(w_up, "dp", axis=0, tiled=True),
         lax.all_gather(w_down, "dp", axis=1, tiled=True),

time: 944 us -> 893 us (0.946)
  waiting for transfers between devices: 649 us -> 586 us
  local copies, waits for them, and re-layouts: 27.1 us -> 40.6 us
    all_gather x2 -> x0, waiting for transfers between devices: 56.2 us -> none  [collect(): lax.all_gather(w_qkv, 'dp', axis=1, tiled=True)]
    all_gather x2, waiting for transfers between devices: 51.6 us -> 0.05 us  [collect(): lax.all_gather(w_up, 'dp', axis=0, tiled=True)]
    ppermute x0 -> x7, waiting for transfers between devices: none -> 50.9 us  [collect_2(): x = lax.ppermute(x, axis, [(d, (d + 1) % ways) for d in range(ways)])]
    dynamic_update_slice x0 -> x16, local copies, waits for them, and re-layouts: none -> 15.2 us  [the longest x14 13.3 us: collect_2(): lax.dynamic_update_slice_in_dim(full, x, (here - far) % ways * hop, axis=...]
  transfers between devices with their start and end apart: 27 -> 32, of which waited for: 26 -> 28; matrix products, arithmetic and copies ran while one was open for 8% -> 11% of each run, Pallas kernels for 0% -> 0%
where the time goes in v1:
time: 893 us; the launch traced here: 891 us
  waiting for transfers between devices  586 us (66%)
  matrix products  131 us (15%)
  blocking collectives  64.6 us (7%)
  other arithmetic  50.3 us (6%)
  local copies, waits for them, and re-layouts  40.6 us (5%)
  between operations  15.7 us (2%)
    unnamed x8, waiting for transfers between devices  73.9 us
    reduce_scatter x2, waiting for transfers between devices, backward(): lax.psum_scatter(jnp.dot(piece, up_w.T, preferred_element_type=jnp.float3...  56.1 us
    all_gather x2, waiting for transfers between devices, collect(): lax.all_gather(w_down, 'dp', axis=1, tiled=True)  54.7 us
    reduce_scatter x2, waiting for transfers between devices, forward(): lax.psum_scatter(jnp.dot(piece, down_w, preferred_element_type=jnp.float3...  53.9 us
    all_gather x2, waiting for transfers between devices, backward(): grad_two_whole = lax.all_gather(grad_two_b, 'tensor', axis=0, tiled=True)  53.2 us
    all_gather x2, waiting for transfers between devices, forward(): normed_whole = lax.all_gather(normed_b, 'tensor', axis=0, tiled=True)  53 us
    reduce_scatter x2, waiting for transfers between devices, forward(): lax.psum_scatter(jnp.dot(piece, out_w, preferred_element_type=jnp.float32...  51.2 us
    ppermute x7, waiting for transfers between devices, collect_2(): x = lax.ppermute(x, axis, [(d, (d + 1) % ways) for d in range(ways)])  50.9 us
  transfers between devices with their start and end apart: 32, of which 28 were waited for; matrix products, arithmetic and copies ran while one was open for 11% of the time, Pallas kernels for 0%

profile of v1, /device:TPU:0, one launch (start us, length us, event | category | flops | bytes accessed | tf_op | source)
XLA Modules:
  0.0 891.5 jit_solution(3127280565707347597)
XLA Ops:
  8.5 7.7 collective-permute-done
  16.2 7.2 collective-permute-done.1
  23.5 7.2 collective-permute-done.2
  30.7 7.2 collective-permute-done.3
  37.9 7.2 collective-permute-done.4
  45.1 7.2 collective-permute-done.5
  52.3 7.2 collective-permute-done.6
  59.5 648.3 %while.25 = (s32[]{:T(128)}, f32[3,1024,256]{1,2,0:T(8,128)}, f32[256,1024]{1,0:T(8,128)}, f32[1024,1024]{1,0:T(8,128)}, f32[1024,1024]{1,0:T(8,128)}, /*index=5...) while((s32[]{:T(128)}, f32[3,1024,256]{1,2,0:T(8,128)}, ...), condition=%wide.region_25.26_spmd.clone, body=%wide.region_0.25_spmd.clone.sunk | while | flops 10544906240 | bytes 277787072 | solution.py:266
  61.3 12.9 %all_gather.66 = bf16[12,1024]{1,0:T(8,128)(2,1)S(1)} all-gather(bf16[12,128]{1,0:T(8,128)(2,1)} %get-tuple-element.780), channel_id=1, replica_groups=mesh['dp'=8,'tensor'=4] {'dp'}, dimensions={1}, use_global_device_ids=true | all-gather | bytes 27648 | tf_op jit(solution)/shard_map/while/body/eval_jaxpr/all_gather | solution.py:62
  83.1 14.3 %all_gather.68 = bf16[256,1024]{1,0:T(8,128)(2,1)S(1)} all-gather(bf16[256,128]{1,0:T(8,128)(2,1)S(1)} %copy-done.23), channel_id=1, replica_groups=mesh['dp'=8,'tensor'=4] {'dp'}, dimensions={1}, use_global_device_ids=true | all-gather | bytes 589824 | tf_op jit(solution)/shard_map/while/body/eval_jaxpr/all_gather | solution.py:59
  97.6 2.2 convolution_bitcast_fusion.3
  105.4 26.3 %reduce-scatter.26.cloned.1.call-done = bf16[128,1024]{1,0:T(8,128)(2,1)} async-done(((bf16[512,1024]{1,0:T(8,128)(2,1)}), bf16[128,1024]{1,0:T(8,128)(2,1)}) %reduce-scatter.26.cloned.1.call-update) | async-done | bytes 262160 | tf_op jit(solution)/shard_map/while/body/eval_jaxpr/reduce_scatter | solution.py:114
  136.5 26.3 %all-gather.15.cloned.1.call-done = bf16[512,1024]{1,0:T(8,128)(2,1)} async-done(((bf16[128,1024]{1,0:T(8,128)(2,1)}), bf16[512,1024]{1,0:T(8,128)(2,1)}) %all-gather.15.cloned.1.call-update) | async-done | bytes 1048592 | tf_op jit(solution)/shard_map/while/body/eval_jaxpr/all_gather | solution.py:123
  162.8 4.5 fusion.165
  167.4 27.4 %all-gather.13.cloned.1.call-done = bf16[1024,1024]{1,0:T(8,128)(2,1)} async-done(((bf16[1024,128]{1,0:T(8,128)(2,1)}), bf16[1024,1024]{1,0:T(8,128)(2,1)}) %all-gather.13.cloned.1.call-update) | async-done | bytes 2097168 | tf_op jit(solution)/shard_map/while/body/eval_jaxpr/all_gather | solution.py:61
  194.7 4.5 convolution_convert_fusion.12
  199.3 27.0 %reduce-scatter.28.cloned.1.call-done = bf16[128,1024]{1,0:T(8,128)(2,1)} async-done(((bf16[512,1024]{1,0:T(8,128)(2,1)}), bf16[128,1024]{1,0:T(8,128)(2,1)}) %reduce-scatter.28.cloned.1.call-update) | async-done | bytes 262160 | tf_op jit(solution)/shard_map/while/body/eval_jaxpr/reduce_scatter | solution.py:130
  230.6 26.6 %all-gather.19.cloned.1.call-done = bf16[512,1024]{1,0:T(8,128)(2,1)} async-done(((bf16[128,1024]{1,0:T(8,128)(2,1)}), bf16[512,1024]{1,0:T(8,128)(2,1)}) %all-gather.19.cloned.1.call-update) | async-done | bytes 1048592 | tf_op jit(solution)/shard_map/while/body/eval_jaxpr/all_gather | solution.py:181
  257.2 4.6 fusion.169
  262.8 2.3 convolution_convert_fusion.13
  265.2 28.0 %reduce-scatter.30.cloned.1.call-done = bf16[128,1024]{1,0:T(8,128)(2,1)} async-done(((bf16[512,1024]{1,0:T(8,128)(2,1)}), bf16[128,1024]{1,0:T(8,128)(2,1)}) %reduce-scatter.30.cloned.1.call-update) | async-done | bytes 262160 | tf_op jit(solution)/shard_map/while/body/eval_jaxpr/reduce_scatter | solution.py:190
  301.2 23.8 %all-gather.21.cloned.1.call-done = bf16[512,1024]{1,0:T(8,128)(2,1)} async-done(((bf16[128,1024]{1,0:T(8,128)(2,1)}), bf16[512,1024]{1,0:T(8,128)(2,1)}) %all-gather.21.cloned.1.call-update) | async-done | bytes 1048592 | tf_op jit(solution)/shard_map/while/body/eval_jaxpr/all_gather | solution.py:201
  326.7 4.1 fusion.171
  330.9 2.9 fusion.172
  333.8 8.1 fusion.173
  341.9 8.8 fusion.174
  350.7 3.6 bitcast_convert_fusion.2
  354.3 3.3 select_add_fusion.6
  357.6 3.3 select_add_fusion.7
  363.7 2.7 convolution_add_fusion.2
  366.5 2.8 bitcast_add_fusion.2
  369.3 13.0 %reduce-scatter.32.cloned.1.call-done = bf16[128,1024]{1,0:T(8,128)(2,1)} async-done(((bf16[512,1024]{1,0:T(8,128)(2,1)}), bf16[128,1024]{1,0:T(8,128)(2,1)}) %reduce-scatter.32.cloned.1.call-update) | async-done | bytes 262160 | tf_op jit(solution)/shard_map/while/body/eval_jaxpr/reduce_scatter | solution.py:230
  386.1 13.0 %all_gather.66 = bf16[12,1024]{1,0:T(8,128)(2,1)S(1)} all-gather(bf16[12,128]{1,0:T(8,128)(2,1)} %get-tuple-element.780), channel_id=1, replica_groups=mesh['dp'=8,'tensor'=4] {'dp'}, dimensions={1}, use_global_device_ids=true | all-gather | bytes 27648 | tf_op jit(solution)/shard_map/while/body/eval_jaxpr/all_gather | solution.py:62
  407.9 13.7 %all_gather.68 = bf16[256,1024]{1,0:T(8,128)(2,1)S(1)} all-gather(bf16[256,128]{1,0:T(8,128)(2,1)S(1)} %copy-done.23), channel_id=1, replica_groups=mesh['dp'=8,'tensor'=4] {'dp'}, dimensions={1}, use_global_device_ids=true | all-gather | bytes 589824 | tf_op jit(solution)/shard_map/while/body/eval_jaxpr/all_gather | solution.py:59
  429.8 24.9 %reduce-scatter.26.cloned.1.call-done = bf16[128,1024]{1,0:T(8,128)(2,1)} async-done(((bf16[512,1024]{1,0:T(8,128)(2,1)}), bf16[128,1024]{1,0:T(8,128)(2,1)}) %reduce-scatter.26.cloned.1.call-update) | async-done | bytes 262160 | tf_op jit(solution)/shard_map/while/body/eval_jaxpr/reduce_scatter | solution.py:114
  459.6 26.7 %all-gather.15.cloned.1.call-done = bf16[512,1024]{1,0:T(8,128)(2,1)} async-done(((bf16[128,1024]{1,0:T(8,128)(2,1)}), bf16[512,1024]{1,0:T(8,128)(2,1)}) %all-gather.15.cloned.1.call-update) | async-done | bytes 1048592 | tf_op jit(solution)/shard_map/while/body/eval_jaxpr/all_gather | solution.py:123
  486.3 4.5 fusion.165
  490.9 27.4 %all-gather.13.cloned.1.call-done = bf16[1024,1024]{1,0:T(8,128)(2,1)} async-done(((bf16[1024,128]{1,0:T(8,128)(2,1)}), bf16[1024,1024]{1,0:T(8,128)(2,1)}) %all-gather.13.cloned.1.call-update) | async-done | bytes 2097168 | tf_op jit(solution)/shard_map/while/body/eval_jaxpr/all_gather | solution.py:61
  518.2 4.5 convolution_convert_fusion.12
  522.8 27.0 %reduce-scatter.28.cloned.1.call-done = bf16[128,1024]{1,0:T(8,128)(2,1)} async-done(((bf16[512,1024]{1,0:T(8,128)(2,1)}), bf16[128,1024]{1,0:T(8,128)(2,1)}) %reduce-scatter.28.cloned.1.call-update) | async-done | bytes 262160 | tf_op jit(solution)/shard_map/while/body/eval_jaxpr/reduce_scatter | solution.py:130
  554.1 26.6 %all-gather.19.cloned.1.call-done = bf16[512,1024]{1,0:T(8,128)(2,1)} async-done(((bf16[128,1024]{1,0:T(8,128)(2,1)}), bf16[512,1024]{1,0:T(8,128)(2,1)}) %all-gather.19.cloned.1.call-update) | async-done | bytes 1048592 | tf_op jit(solution)/shard_map/while/body/eval_jaxpr/all_gather | solution.py:181
  580.7 4.6 fusion.169
  586.2 2.3 convolution_convert_fusion.13
  588.6 28.0 %reduce-scatter.30.cloned.1.call-done = bf16[128,1024]{1,0:T(8,128)(2,1)} async-done(((bf16[512,1024]{1,0:T(8,128)(2,1)}), bf16[128,1024]{1,0:T(8,128)(2,1)}) %reduce-scatter.30.cloned.1.call-update) | async-done | bytes 262160 | tf_op jit(solution)/shard_map/while/body/eval_jaxpr/reduce_scatter | solution.py:190
  624.7 23.8 %all-gather.21.cloned.1.call-done = bf16[512,1024]{1,0:T(8,128)(2,1)} async-done(((bf16[128,1024]{1,0:T(8,128)(2,1)}), bf16[512,1024]{1,0:T(8,128)(2,1)}) %all-gather.21.cloned.1.call-update) | async-done | bytes 1048592 | tf_op jit(solution)/shard_map/while/body/eval_jaxpr/all_gather | solution.py:201
  650.2 4.1 fusion.171
  654.4 2.9 fusion.172
  657.2 8.1 fusion.173
  665.3 8.8 fusion.174
  674.1 3.6 bitcast_convert_fusion.2
  677.8 5.6 select_add_fusion.6
  683.4 5.7 select_add_fusion.7
  691.9 3.1 convolution_add_fusion.2
  695.0 2.8 bitcast_add_fusion.2
  697.8 8.0 reduce-scatter.32.cloned.1.call-done
  714.8 2.5 convert_element_type.199
  717.4 2.6 copy.37
  720.1 3.9 convert_element_type.197
  724.0 17.9 %reduce-scatter.24.cloned.1.call-done = bf16[128,12]{1,0:T(8,128)(2,1)} async-done(((bf16[1024,12]{1,0:T(8,128)(2,1)}), bf16[128,12]{1,0:T(8,128)(2,1)}) %reduce-scatter.24.cloned.1.call-update) | async-done | bytes 3088
  742.7 10.6 %psum.7 = f32[12,128]{1,0:T(8,128)} all-reduce(bf16[12,128]{1,0:T(8,128)(2,1)S(1)} %copy.40), channel_id=1, replica_groups=mesh['dp'=8,'tensor'=4] {'tensor'}, use_global_device_ids=true, to_apply=%region_31.32 | all-reduce | flops 1536 | bytes 9216 | tf_op jit(solution)/shard_map/psum | solution.py:268
  753.3 20.9 %reduce-scatter.20.cloned.1.call-done = bf16[128,256]{1,0:T(8,128)(2,1)} async-done(((bf16[1024,256]{1,0:T(8,128)(2,1)}), bf16[128,256]{1,0:T(8,128)(2,1)}) %reduce-scatter.20.cloned.1.call-update) | async-done | bytes 65552
  775.8 32.9 %reduce-scatter.16.cloned.1.call-done = bf16[3,128,256]{2,1,0:T(8,128)(2,1)} async-done(((bf16[3,1024,256]{2,1,0:T(8,128)(2,1)}), bf16[3,128,256]{2,1,0:T(8,128)(2,1)}) %reduce-scatter.16.cloned.1.call-update) | async-done | bytes 196624 | tf_op jit(solution)/shard_map/reduce_scatter | solution.py:68
  810.4 35.1 %reduce-scatter.22.cloned.1.call-done = bf16[128,1024]{1,0:T(8,128)(2,1)} async-done(((bf16[1024,1024]{1,0:T(8,128)(2,1)}), bf16[128,1024]{1,0:T(8,128)(2,1)}) %reduce-scatter.22.cloned.1.call-update) | async-done | bytes 262160
  847.5 34.6 %reduce-scatter.18.cloned.1.call-done = bf16[128,1024]{1,0:T(8,128)(2,1)} async-done(((bf16[1024,1024]{1,0:T(8,128)(2,1)}), bf16[128,1024]{1,0:T(8,128)(2,1)}) %reduce-scatter.18.cloned.1.call-update) | async-done | bytes 262160 | tf_op jit(solution)/shard_map/reduce_scatter | solution.py:74
  (327 shorter events, 99.2 us)
Async XLA Ops:
  8.0 8.2 collective-permute-start
  16.2 7.2 collective-permute-start.1
  23.5 7.2 collective-permute-start.2
  30.7 7.2 collective-permute-start.3
  37.9 7.2 collective-permute-start.4
  45.1 7.2 collective-permute-start.5
  52.3 7.2 collective-permute-start.6
  59.5 23.6 %copy-start.23 = (bf16[256,128]{1,0:T(8,128)(2,1)S(1)}, bf16[256,128]{1,0:T(8,128)(2,1)}, u32[]{:S(2)}) copy-start(bf16[256,128]{1,0:T(8,128)(2,1)} %get-tuple-element.782) | copy-start | bytes 196612 | tf_op jit(solution)/shard_map/while
  59.5 38.1 %all-gather.11.cloned.1.call-start = ((), (), s32[]{:S(2)}) async-start(), calls=%async_computation.14 | async-start | bytes 1310720 | tf_op jit(solution)/shard_map/while/body/eval_jaxpr/all_gather | solution.py:97
  61.2 70.4 %reduce-scatter.26.cloned.1.call-start = ((), (), s32[]{:S(2)}) async-start(), calls=%async_computation.16 | async-start | bytes 1310720 | tf_op jit(solution)/shard_map/while/body/eval_jaxpr/reduce_scatter | solution.py:114
  74.5 27.4 %copy-start.27 = (f32[4,64]{1,0:T(4,128)}, f32[4,64]{1,0:T(4,128)S(1)}, u32[]{:S(2)}) copy-start(f32[4,64]{1,0:T(4,128)S(1)} %add.705) | copy-start | bytes 3076 | tf_op jit(solution)/shard_map/while
  74.6 25.4 %copy-start.25 = (f32[4,64]{1,0:T(4,128)}, f32[4,64]{1,0:T(4,128)S(1)}, u32[]{:S(2)}) copy-start(f32[4,64]{1,0:T(4,128)S(1)} %add.706) | copy-start | bytes 3076 | tf_op jit(solution)/shard_map/while
  83.1 16.8 %copy-start.11 = (bf16[3,1024,256]{2,1,0:T(8,128)(2,1)}, bf16[3,1024,256]{2,1,0:T(8,128)(2,1)S(1)}, u32[]{:S(2)}) copy-start(bf16[3,1024,256]{2,1,0:T(8,128)(2,1)S(1)} %constant_dynamic-update-slice_fusion.27) | copy-start | bytes 4718596 | tf_op jit(solution)/shard_map/while
  101.9 29.7 %copy-start.5 = (bf16[2,128,1024]{2,1,0:T(8,128)(2,1)S(1)}, bf16[2,128,1024]{2,1,0:T(8,128)(2,1)}, u32[]{:S(2)}) copy-start(bf16[2,128,1024]{2,1,0:T(8,128)(2,1)} %get-tuple-element.778) | copy-start | bytes 1572868 | tf_op jit(solution)/shard_map/while
  104.7 31.8 %all-gather.17.cloned.1.call-start = ((), (), s32[]{:S(2)}) async-start(), calls=%async_computation.18 | async-start | bytes 2359296 | tf_op jit(solution)/shard_map/while/body/eval_jaxpr/all_gather | solution.py:60
  105.3 57.5 %all-gather.15.cloned.1.call-start = ((), (), s32[]{:S(2)}) async-start(), calls=%async_computation.17 | async-start | bytes 1310720 | tf_op jit(solution)/shard_map/while/body/eval_jaxpr/all_gather | solution.py:123
  135.8 58.9 %all-gather.13.cloned.1.call-start = ((), (), s32[]{:S(2)}) async-start(), calls=%async_computation.15 | async-start | bytes 2359296 | tf_op jit(solution)/shard_map/while/body/eval_jaxpr/all_gather | solution.py:61
  136.4 89.9 %reduce-scatter.28.cloned.1.call-start = ((), (), s32[]{:S(2)}) async-start(), calls=%async_computation.19 | async-start | bytes 1310720 | tf_op jit(solution)/shard_map/while/body/eval_jaxpr/reduce_scatter | solution.py:130
  167.4 58.9 %copy-start.1 = (bf16[128,1024]{1,0:T(8,128)(2,1)S(1)}, bf16[128,1024]{1,0:T(8,128)(2,1)}, u32[]{:S(2)}) copy-start(bf16[128,1024]{1,0:T(8,128)(2,1)} %reduce-scatter.26.cloned.1.call-done) | copy-start | bytes 786436 | tf_op jit(solution)/shard_map/while
  167.4 60.4 %copy-start.12 = (bf16[2,128,1024]{2,1,0:T(8,128)(2,1)S(1)}, bf16[2,128,1024]{2,1,0:T(8,128)(2,1)}, u32[]{:S(2)}) copy-start(bf16[2,128,1024]{2,1,0:T(8,128)(2,1)} %get-tuple-element.786) | copy-start | bytes 1572868 | tf_op jit(solution)/shard_map/while
  199.3 57.9 %all-gather.19.cloned.1.call-start = ((), (), s32[]{:S(2)}) async-start(), calls=%async_computation.20 | async-start | bytes 1310720 | tf_op jit(solution)/shard_map/while/body/eval_jaxpr/all_gather | solution.py:181
  230.5 62.7 %reduce-scatter.30.cloned.1.call-start = ((), (), s32[]{:S(2)}) async-start(), calls=%async_computation.21 | async-start | bytes 1310720 | tf_op jit(solution)/shard_map/while/body/eval_jaxpr/reduce_scatter | solution.py:190
  257.2 5.6 copy-start.31
  265.1 59.9 %all-gather.21.cloned.1.call-start = ((), (), s32[]{:S(2)}) async-start(), calls=%async_computation.22 | async-start | bytes 1310720 | tf_op jit(solution)/shard_map/while/body/eval_jaxpr/all_gather | solution.py:201
  295.1 31.6 %copy-start.30 = (f32[4,512]{1,0:T(4,128)S(1)}, f32[4,512]{1,0:T(4,128)}, u32[]{:S(2)}) copy-start(f32[4,512]{1,0:T(4,128)} %copy-done.29) | copy-start | bytes 24580 | tf_op jit(solution)/shard_map/while
  298.5 83.9 %reduce-scatter.32.cloned.1.call-start = ((), (), s32[]{:S(2)}) async-start(), calls=%async_computation.23 | async-start | bytes 1310720 | tf_op jit(solution)/shard_map/while/body/eval_jaxpr/reduce_scatter | solution.py:230
  326.7 4.2 copy-start.9
  333.8 8.1 copy-start.16
  341.8 8.8 copy-start.18
  341.8 8.8 copy-start.20
  360.9 5.5 copy-start.2
  369.3 15.0 %copy-start.3 = (f32[3,1024,256]{1,2,0:T(8,128)}, f32[3,1024,256]{1,2,0:T(8,128)S(1)}, u32[]{:S(2)}) copy-start(f32[3,1024,256]{1,2,0:T(8,128)S(1)} %bitcast_add_fusion.2) | copy-start | bytes 9437188 | tf_op jit(solution)/shard_map/while
  384.3 23.6 %copy-start.23 = (bf16[256,128]{1,0:T(8,128)(2,1)S(1)}, bf16[256,128]{1,0:T(8,128)(2,1)}, u32[]{:S(2)}) copy-start(bf16[256,128]{1,0:T(8,128)(2,1)} %get-tuple-element.782) | copy-start | bytes 196612 | tf_op jit(solution)/shard_map/while
  384.3 37.6 %all-gather.11.cloned.1.call-start = ((), (), s32[]{:S(2)}) async-start(), calls=%async_computation.14 | async-start | bytes 1310720 | tf_op jit(solution)/shard_map/while/body/eval_jaxpr/all_gather | solution.py:97
  386.1 68.6 %reduce-scatter.26.cloned.1.call-start = ((), (), s32[]{:S(2)}) async-start(), calls=%async_computation.16 | async-start | bytes 1310720 | tf_op jit(solution)/shard_map/while/body/eval_jaxpr/reduce_scatter | solution.py:114
  399.4 26.8 %copy-start.27 = (f32[4,64]{1,0:T(4,128)}, f32[4,64]{1,0:T(4,128)S(1)}, u32[]{:S(2)}) copy-start(f32[4,64]{1,0:T(4,128)S(1)} %add.705) | copy-start | bytes 3076 | tf_op jit(solution)/shard_map/while
  399.5 24.8 %copy-start.25 = (f32[4,64]{1,0:T(4,128)}, f32[4,64]{1,0:T(4,128)S(1)}, u32[]{:S(2)}) copy-start(f32[4,64]{1,0:T(4,128)S(1)} %add.706) | copy-start | bytes 3076 | tf_op jit(solution)/shard_map/while
  407.9 16.3 %copy-start.11 = (bf16[3,1024,256]{2,1,0:T(8,128)(2,1)}, bf16[3,1024,256]{2,1,0:T(8,128)(2,1)S(1)}, u32[]{:S(2)}) copy-start(bf16[3,1024,256]{2,1,0:T(8,128)(2,1)S(1)} %constant_dynamic-update-slice_fusion.27) | copy-start | bytes 4718596 | tf_op jit(solution)/shard_map/while
  426.2 28.5 %copy-start.5 = (bf16[2,128,1024]{2,1,0:T(8,128)(2,1)S(1)}, bf16[2,128,1024]{2,1,0:T(8,128)(2,1)}, u32[]{:S(2)}) copy-start(bf16[2,128,1024]{2,1,0:T(8,128)(2,1)} %get-tuple-element.778) | copy-start | bytes 1572868 | tf_op jit(solution)/shard_map/while
  429.0 30.5 %all-gather.17.cloned.1.call-start = ((), (), s32[]{:S(2)}) async-start(), calls=%async_computation.18 | async-start | bytes 2359296 | tf_op jit(solution)/shard_map/while/body/eval_jaxpr/all_gather | solution.py:60
  429.8 56.5 %all-gather.15.cloned.1.call-start = ((), (), s32[]{:S(2)}) async-start(), calls=%async_computation.17 | async-start | bytes 1310720 | tf_op jit(solution)/shard_map/while/body/eval_jaxpr/all_gather | solution.py:123
  458.8 59.4 %all-gather.13.cloned.1.call-start = ((), (), s32[]{:S(2)}) async-start(), calls=%async_computation.15 | async-start | bytes 2359296 | tf_op jit(solution)/shard_map/while/body/eval_jaxpr/all_gather | solution.py:61
  459.4 90.4 %reduce-scatter.28.cloned.1.call-start = ((), (), s32[]{:S(2)}) async-start(), calls=%async_computation.19 | async-start | bytes 1310720 | tf_op jit(solution)/shard_map/while/body/eval_jaxpr/reduce_scatter | solution.py:130
  490.8 58.9 %copy-start.1 = (bf16[128,1024]{1,0:T(8,128)(2,1)S(1)}, bf16[128,1024]{1,0:T(8,128)(2,1)}, u32[]{:S(2)}) copy-start(bf16[128,1024]{1,0:T(8,128)(2,1)} %reduce-scatter.26.cloned.1.call-done) | copy-start | bytes 786436 | tf_op jit(solution)/shard_map/while
  490.9 60.4 %copy-start.12 = (bf16[2,128,1024]{2,1,0:T(8,128)(2,1)S(1)}, bf16[2,128,1024]{2,1,0:T(8,128)(2,1)}, u32[]{:S(2)}) copy-start(bf16[2,128,1024]{2,1,0:T(8,128)(2,1)} %get-tuple-element.786) | copy-start | bytes 1572868 | tf_op jit(solution)/shard_map/while
  522.8 57.9 %all-gather.19.cloned.1.call-start = ((), (), s32[]{:S(2)}) async-start(), calls=%async_computation.20 | async-start | bytes 1310720 | tf_op jit(solution)/shard_map/while/body/eval_jaxpr/all_gather | solution.py:181
  554.0 62.7 %reduce-scatter.30.cloned.1.call-start = ((), (), s32[]{:S(2)}) async-start(), calls=%async_computation.21 | async-start | bytes 1310720 | tf_op jit(solution)/shard_map/while/body/eval_jaxpr/reduce_scatter | solution.py:190
  580.7 5.6 copy-start.31
  588.6 59.9 %all-gather.21.cloned.1.call-start = ((), (), s32[]{:S(2)}) async-start(), calls=%async_computation.22 | async-start | bytes 1310720 | tf_op jit(solution)/shard_map/while/body/eval_jaxpr/all_gather | solution.py:201
  618.6 31.6 %copy-start.30 = (f32[4,512]{1,0:T(4,128)S(1)}, f32[4,512]{1,0:T(4,128)}, u32[]{:S(2)}) copy-start(f32[4,512]{1,0:T(4,128)} %copy-done.29) | copy-start | bytes 24580 | tf_op jit(solution)/shard_map/while
  622.0 83.9 %reduce-scatter.32.cloned.1.call-start = ((), (), s32[]{:S(2)}) async-start(), calls=%async_computation.23 | async-start | bytes 1310720 | tf_op jit(solution)/shard_map/while/body/eval_jaxpr/reduce_scatter | solution.py:230
  657.2 8.1 copy-start.16
  665.3 8.8 copy-start.18
  665.3 8.8 copy-start.20
  677.8 5.6 copy-start.10
  677.8 5.6 copy-start.17
  689.1 5.9 copy-start.2
  697.8 10.0 %copy-start.3 = (f32[3,1024,256]{1,2,0:T(8,128)}, f32[3,1024,256]{1,2,0:T(8,128)S(1)}, u32[]{:S(2)}) copy-start(f32[3,1024,256]{1,2,0:T(8,128)S(1)} %bitcast_add_fusion.2) | copy-start | bytes 9437188 | tf_op jit(solution)/shard_map/while
  707.8 5.3 copy-start.4
  707.8 34.0 %reduce-scatter.24.cloned.1.call-start = ((), (), s32[]{:S(2)}) async-start(), calls=%async_computation.13 | async-start | bytes 294912
  708.8 65.4 %reduce-scatter.20.cloned.1.call-start = ((), (), s32[]{:S(2)}) async-start(), calls=%async_computation.11 | async-start | bytes 589824
  713.0 95.7 %reduce-scatter.16.cloned.1.call-start = ((), (), s32[]{:S(2)}) async-start(), calls=%async_computation.9 | async-start | bytes 1769472 | tf_op jit(solution)/shard_map/reduce_scatter | solution.py:68
  714.8 130.7 %reduce-scatter.22.cloned.1.call-start = ((), (), s32[]{:S(2)}) async-start(), calls=%async_computation.12 | async-start | bytes 2359296
  720.0 162.1 %reduce-scatter.18.cloned.1.call-start = ((), (), s32[]{:S(2)}) async-start(), calls=%async_computation.10 | async-start | bytes 2359296 | tf_op jit(solution)/shard_map/reduce_scatter | solution.py:74
  (31 other events, 79.3 us)
Sparse Core Ops, SparseCore 0:
  62.7 25.1 all-gather.10
  104.8 26.7 reduce-scatter.25
  199.4 26.8 reduce-scatter.27
  230.7 26.4 all-gather.18
  265.2 27.9 reduce-scatter.29
  354.4 27.9 reduce-scatter.31
  387.5 26.4 all-gather.10
  429.1 25.5 reduce-scatter.25
  522.9 26.8 reduce-scatter.27
  554.1 26.4 all-gather.18
  588.7 27.9 reduce-scatter.29
  677.9 27.9 reduce-scatter.31
Sparse Core Ops, SparseCore 1:
  106.8 27.9 all-gather.16
  137.1 25.7 all-gather.14
  164.3 30.4 all-gather.12
  298.6 26.3 all-gather.20
  431.4 26.6 all-gather.16
  460.6 25.7 all-gather.14
  487.8 30.4 all-gather.12
  622.1 26.3 all-gather.20
  711.1 30.7 reduce-scatter.23
  744.7 29.4 reduce-scatter.19
  776.4 32.3 reduce-scatter.15
  811.1 34.4 reduce-scatter.21
  847.7 34.4 reduce-scatter.17
